TPU v7x, 32 devices: a whole 2x2x4 slice. The times are simulated.
32 devices in a mesh: gx: 2 (over y), gy: 4 (over x, core), gz: 4 (over z).
Axes of the slice: x: 2, y: 2, z: 4, core: 2. Of those that a mesh axis runs over, the one named last changes fastest.
Arguments:
- targets: float32 [512, 512, 512], P('gx', 'gy', 'gz'), may hold values from -6 to 6
- basis_first: float32 [512, 512], replicated, may hold values from -0.25 to 0.25
- basis_second: float32 [512, 512], replicated, may hold values from -0.25 to 0.25
- basis_third: float32 [512, 512], replicated, may hold values from -0.25 to 0.25
- eigen_first: float32 [512], replicated, may hold values from 0.1 to 1
- eigen_second: float32 [512], replicated, may hold values from 0.1 to 1
- eigen_third: float32 [512], replicated, may hold values from 0.1 to 1
- noise: float32 [1], replicated, may hold values from 0.5 to 1
Outputs:
- weights: float32 [512, 512, 512], P('gx', 'gy', 'gz')
All inputs are finite; a program needn't handle non-finite values.
Results may differ from a plain program's by a relative error of at most 0.000071.
Values sent between devices are 32-bit elements; how exact they have to be, the bound alone decides.
A program may use at most 128 MiB of HBM per device.

v0:
```python
import jax
import jax.numpy as jnp
from jax import lax
from jax.sharding import PartitionSpec as P


def per_device(
    targets, basis_first, basis_second, basis_third, eigen_first, eigen_second, eigen_third, noise
):
    high = lax.Precision.HIGHEST
    count_z = lax.axis_size("gz")
    full_one = basis_first.shape[0]
    full_three = basis_third.shape[0]
    block = lax.all_to_all(targets, "gz", split_axis=0, concat_axis=2, tiled=True)
    lead, middle = (block.shape[0], block.shape[1])
    block = jnp.dot(block.reshape(-1, full_three), basis_third, precision=high).reshape(
        lead, middle, full_three
    )
    block = lax.all_to_all(block, "gy", split_axis=2, concat_axis=1, tiled=True)
    block = jnp.einsum("ajc,jb->abc", block, basis_second, precision=high)
    block = lax.all_to_all(block, ("gx", "gz"), split_axis=1, concat_axis=0, tiled=True)
    width_two, width_three = (block.shape[1], block.shape[2])
    flat = block.reshape(full_one, -1)
    rotated = jnp.dot(basis_first.T, flat, precision=high).reshape(full_one, width_two, width_three)
    start_two = (lax.axis_index("gx") * count_z + lax.axis_index("gz")) * width_two
    start_three = lax.axis_index("gy") * width_three
    local_two = lax.dynamic_slice_in_dim(eigen_second, start_two, width_two, 0)
    local_three = lax.dynamic_slice_in_dim(eigen_third, start_three, width_three, 0)
    spectrum = (
        eigen_first[:, None, None] * local_two[None, :, None] * local_three[None, None, :]
        + noise[0]
    )
    scaled = rotated / spectrum
    result = jnp.dot(basis_first, scaled.reshape(full_one, -1), precision=high).reshape(
        full_one, width_two, width_three
    )
    result = lax.all_to_all(result, ("gx", "gz"), split_axis=0, concat_axis=1, tiled=True)
    result = jnp.einsum("abc,jb->ajc", result, basis_second, precision=high)
    result = lax.all_to_all(result, "gy", split_axis=1, concat_axis=2, tiled=True)
    lead, middle = (result.shape[0], result.shape[1])
    result = jnp.dot(result.reshape(-1, full_three), basis_third.T, precision=high).reshape(
        lead, middle, full_three
    )
    return lax.all_to_all(result, "gz", split_axis=2, concat_axis=0, tiled=True)


def solution(mesh):
    return jax.shard_map(
        per_device,
        mesh=mesh,
        in_specs=(P("gx", "gy", "gz"), P(), P(), P(), P(), P(), P(), P()),
        out_specs=P("gx", "gy", "gz"),
        check_vma=False,
    )
```

profile of v0, /device:TPU:0, one launch (start us, length us, event | category | flops | bytes accessed | tf_op | source)
XLA Modules:
  0.0 2318.1 jit_solution(12663117489920106023)
XLA Ops:
  0.0 0.0 copy-start
  0.0 369.4 %all_to_all.99 = f32[256,128,128]{2,1,0:T(8,128)S(1)} all-to-all(f32[256,128,128]{2,1,0:T(8,128)} %param.8), channel_id=1, replica_groups=mesh['gx'=2,'gy'=4,'gz'=4] {'gz'}, dimensions={0} | all-to-all | bytes 33554432 | tf_op jit(solution)/shard_map/all_to_all | solution.py:14
  369.4 11.8 copy.50
  381.2 0.0 copy-start.3
  381.2 20.0 dot_general.26
  401.2 0.0 copy-done.3
  401.2 31.8 %fusion.11 = f32[64,128,512]{2,1,0:T(8,128)} fusion(f32[64,128,512]{2,1,0:T(8,128)} %dot_general.26, f32[512,512]{1,0:T(8,128)S(1)} %copy-done.3), kind=kOutput, calls=%fused_computation.15 | convolution fusion | flops 25769803776 | bytes 34603008 | tf_op jit(solution)/shard_map/dot_general | solution.py:16
  433.0 16.6 copy.24
  449.6 187.9 %all_to_all.100 = f32[64,128,512]{1,0,2:T(8,128)S(1)} all-to-all(f32[64,128,512]{1,0,2:T(8,128)} %copy.24), channel_id=1, replica_groups=mesh['gx'=2,'gy'=4,'gz'=4] {'gy'}, dimensions={2} | all-to-all | bytes 33554432 | tf_op jit(solution)/shard_map/all_to_all | solution.py:19
  637.5 18.7 copy.49
  656.2 0.0 copy-start.2
  656.2 20.0 all_to_all.78
  676.2 0.0 copy-done.2
  676.2 31.8 %convolution_bitcast_fusion.1 = f32[64,512,128]{1,2,0:T(8,128)} fusion(f32[64,512,128]{1,2,0:T(8,128)} %all_to_all.78, f32[512,512]{1,0:T(8,128)S(1)} %copy-done.2), kind=kOutput, calls=%fused_computation.10 | convolution fusion | flops 25769803776 | bytes 34603008 | tf_op jit(solution)/shard_map/ajc,jb->abc/dot_general | solution.py:20
  708.0 16.5 copy.26
  724.5 0.0 copy-start.5
  724.5 6.3 all-to-all-start.2
  731.5 0.8 dynamic_slice.7
  732.2 0.8 dynamic_slice.6
  733.0 0.0 copy-done.5
  733.0 0.1 broadcast_multiply_fusion
  733.1 361.3 %all-to-all-done.2 = f32[64,512,128]{2,0,1:T(8,128)} async-done(((f32[64,512,128]{2,0,1:T(8,128)}), f32[64,512,128]{2,0,1:T(8,128)}, u32[]{:S(2)}, u32[]{:S(2)}) %all-to-all-start.2) | async-done | bytes 16777248 | tf_op jit(solution)/shard_map/all_to_all | solution.py:21
  1094.4 17.7 copy.28
  1112.1 0.0 copy-done
  1112.2 40.2 %fusion.4 = f32[512,8192]{0,1:T(8,128)S(1)} fusion(f32[512,512]{1,0:T(8,128)S(1)} %copy-done, f32[64,8,64,128]{3,2,1,0:T(8,128)} %bitcast.70, f32[]{:T(128)} %bitcast.67, f32[8192]{0:T(1024)S(1)} %broadcast_bitcast_fusion, f32[512,64]{0,1:T(8,128)S(1)} %broadcast_multiply_fusion), kind=kOutput, calls=%fused_computation.5 | convolution fusion | flops 25782386688 | bytes 34766852 | tf_op jit(solution)/shard_map/dot_general | solution.py:24
  1152.4 30.3 %fusion.13 = f32[8192,512]{1,0:T(8,128)} fusion(f32[512,8192]{0,1:T(8,128)S(1)} %fusion.4, f32[512,512]{1,0:T(8,128)S(1)} %copy-done), kind=kOutput, calls=%fused_computation.19 | convolution fusion | flops 25769803776 | bytes 34603008 | tf_op jit(solution)/shard_map/dot_general | solution.py:34
  1182.7 16.6 copy.29
  1199.2 371.2 %all_to_all.101 = f32[512,64,128]{2,1,0:T(8,128)} all-to-all(f32[512,64,128]{2,1,0:T(8,128)} %copy.29), channel_id=1, replica_groups=mesh['gx'=2,'gy'=4,'gz'=4] {'gx','gz'}, dimensions={0} | all-to-all | bytes 33554432 | tf_op jit(solution)/shard_map/all_to_all | solution.py:37
  1570.4 6.6 copy.30
  1577.0 58.9 %convolution_bitcast_fusion = f32[64,512,128]{1,2,0:T(8,128)} fusion(f32[64,512,128]{2,1,0:T(8,128)S(1)} %bitcast.68, f32[512,512]{1,0:T(8,128)S(1)} %copy-done.2), kind=kOutput, calls=%fused_computation.9 | convolution fusion | flops 25769803776 | bytes 34603008 | tf_op jit(solution)/shard_map/abc,jb->ajc/dot_general | solution.py:38
  1635.9 16.6 copy.32
  1652.5 187.7 %all_to_all.102 = f32[64,512,128]{2,0,1:T(8,128)S(1)} all-to-all(f32[64,512,128]{2,0,1:T(8,128)} %copy.32), channel_id=1, replica_groups=mesh['gx'=2,'gy'=4,'gz'=4] {'gy'}, dimensions={1} | all-to-all | bytes 33554432 | tf_op jit(solution)/shard_map/all_to_all | solution.py:39
  1840.1 18.7 copy.48
  1858.9 0.0 copy-start.4
  1858.9 20.0 dot_general.34
  1878.8 0.0 copy-done.4
  1878.8 31.8 %fusion.9 = f32[64,128,512]{2,1,0:T(8,128)} fusion(f32[64,128,512]{2,1,0:T(8,128)} %dot_general.34, f32[512,512]{1,0:T(8,128)S(1)} %copy-done.4), kind=kOutput, calls=%fused_computation.13 | convolution fusion | flops 25769803776 | bytes 34603008 | tf_op jit(solution)/shard_map/dot_general | solution.py:41
  1910.7 16.6 copy.34
  1927.2 373.8 %all_to_all.103 = f32[64,128,512]{1,0,2:T(8,128)} all-to-all(f32[64,128,512]{1,0,2:T(8,128)} %copy.34), channel_id=1, replica_groups=mesh['gx'=2,'gy'=4,'gz'=4] {'gz'}, dimensions={2} | all-to-all | bytes 33554432 | tf_op jit(solution)/shard_map/all_to_all | solution.py:44
  2301.0 0.0 copy-start.1
  2301.0 16.6 copy.35
  2317.7 0.0 copy-done.1
  (1 shorter events, 0.0 us)
Async XLA Ops:
  0.0 1112.2 %copy-start = (f32[512,512]{1,0:T(8,128)S(1)}, f32[512,512]{1,0:T(8,128)}, u32[]{:S(2)}) copy-start(f32[512,512]{1,0:T(8,128)} %param.9) | copy-start | bytes 3145732
  381.2 20.0 copy-start.3
  656.2 20.0 copy-start.2
  724.5 8.5 copy-start.5
  724.5 369.9 %all-to-all-start.2 = ((f32[64,512,128]{2,0,1:T(8,128)}), f32[64,512,128]{2,0,1:T(8,128)}, u32[]{:S(2)}, u32[]{:S(2)}) async-start(f32[64,512,128]{2,0,1:T(8,128)} %copy.26), calls=%async_computation.2 | async-start | bytes 33554432 | tf_op jit(solution)/shard_map/all_to_all | solution.py:21
  1858.9 20.0 copy-start.4
  2301.0 16.6 copy-start.1
where the time goes:
time: 2330 us; the launch traced here: 2320 us
  blocking collectives  1490 us (64%)
  waiting for transfers between devices  361 us (15%)
  local copies, waits for them, and re-layouts  235 us (10%)
  matrix products  225 us (10%)
    all_to_all x1, blocking collectives, per_device(): return lax.all_to_all(result, 'gz', split_axis=2, concat_axis=0, tiled=True)  374 us
    all_to_all x1, blocking collectives, per_device(): lax.all_to_all(result, ('gx', 'gz'), split_axis=0, concat_axis=1, tiled=T...  371 us
    all_to_all x1, blocking collectives, per_device(): lax.all_to_all(targets, 'gz', split_axis=0, concat_axis=2, tiled=True)  369 us
    all_to_all x1, waiting for transfers between devices, per_device(): lax.all_to_all(block, ('gx', 'gz'), split_axis=1, concat_axis=0, tiled=True)  361 us
    all_to_all x1, blocking collectives, per_device(): block = lax.all_to_all(block, 'gy', split_axis=2, concat_axis=1, tiled=True)  188 us
    all_to_all x1, blocking collectives, per_device(): lax.all_to_all(result, 'gy', split_axis=1, concat_axis=2, tiled=True)  188 us
    dot_general x1, matrix products, per_device(): result = jnp.einsum('abc,jb->ajc', result, basis_second, precision=high)  58.9 us
  transfers between devices with their start and end apart: 1, of which 1 were waited for; matrix products, arithmetic and copies ran while one was open for 0% of the time, Pallas kernels for 0%

commit v1 on v0

v1 whole, which is shorter than its diff:
```python
import jax
import jax.numpy as jnp
from jax import lax
from jax.experimental import pallas as pl
from jax.experimental.pallas import tpu as pltpu
from jax.sharding import PartitionSpec as P

MESH = pl.DeviceIdType.MESH
CHUNKS = 4
HIGH = lax.Precision.HIGH


def offsets_of(sizes, names):
    found = [{}]
    for name in names:
        found = [{**base, name: step} for base in found for step in range(sizes[name])]
    found = [one for one in found if any(one.values())]
    far = lambda one: min(one.get("gz", 0), sizes["gz"] - one.get("gz", 0))
    return sorted(found, key=lambda one: -far(one))


def kernel(sizes, tasks, n_in, fresh, *refs):
    ins, outs, sems = refs[:n_in], refs[n_in:-1 - 2 * len(tasks)], refs[-1 - 2 * len(tasks):]
    me = {name: lax.axis_index(name) for name in sizes}
    everyone = "gz" if any("gz" in task[1] for task in tasks) else ""
    reach = ("gz", "gx", "gy") if everyone else ("gx", "gy")
    shift = lambda off: {n: (lax.rem(me[n] + s, sizes[n]) if s else me[n]) for n, s in off.items()}

    barrier = pltpu.get_barrier_semaphore()
    greeted = offsets_of(sizes, reach)
    for off in greeted:
        pl.semaphore_signal(barrier, inc=1, device_id=shift(off), device_id_type=MESH)
    pl.semaphore_wait(barrier, len(greeted))

    def rank(where, names):
        total = 0
        for n in names:
            total = total * sizes[n] + where[n]
        return total

    def parts(task, source, target, where_from, where_to):
        gathers, names, first, depth = task[0], task[1], task[4], task[5]
        grid, spine = (target, source) if gathers else (source, target)
        holder = where_from if gathers else where_to
        other = where_to if gathers else where_from
        rows, cols = spine.shape[1], spine.shape[2]
        run = spine.shape[0] // max(1, _count(sizes, names))
        k_at = rank(other, names) * run + first
        spine_part = spine.at[pl.ds(k_at, depth)]
        row_at = pl.multiple_of(rank(holder, names[:-1]) * rows, 8)
        col_at = pl.multiple_of(rank(holder, names[-1:]) * cols, 128)
        grid_part = grid.at[:, pl.ds(row_at, rows), pl.ds(col_at, cols)]
        return (spine_part, grid_part) if gathers else (grid_part, spine_part)

    running = []
    for t, task in enumerate(tasks):
        source = ins[task[2]]
        target = outs[task[3]]
        send, recv = sems[2 * t], sems[2 * t + 1]
        for s, off in enumerate(offsets_of(sizes, task[1])):
            peer = shift(off)
            src, dst = parts(task, source, target, me, peer)
            copy = pltpu.make_async_remote_copy(
                src_ref=src, dst_ref=dst, send_sem=send.at[s], recv_sem=recv.at[s],
                device_id=peer, device_id_type=MESH,
            )
            copy.start()
            running.append(copy)
        src, dst = parts(task, source, target, me, me)
        own = pltpu.make_async_copy(src, dst, sems[-1].at[t])
        own.start()
        running.append(own)
    for copy in running:
        copy.wait()


def _count(sizes, names):
    total = 1
    for n in names:
        total *= sizes[n]
    return total


def exchange(sizes, cid, tasks, sources, shapes, carried=None):
    carried = carried or {}
    n_src = len(sources)
    aliases = {n_src + i: out for i, out in enumerate(sorted(carried))}
    extra = [carried[out] for out in sorted(carried)]
    scratch = []
    for task in tasks:
        n = _count(sizes, task[1]) - 1
        scratch += [pltpu.SemaphoreType.DMA((n,)), pltpu.SemaphoreType.DMA((n,))]
    scratch.append(pltpu.SemaphoreType.DMA((len(tasks),)))
    any_space = pl.BlockSpec(memory_space=pl.ANY)

    def body(*refs):
        kernel(sizes, tasks, n_src + len(extra), None, *refs)

    return pl.pallas_call(
        body,
        out_shape=[jax.ShapeDtypeStruct(s, jnp.float32) for s in shapes],
        in_specs=[any_space] * (n_src + len(extra)),
        out_specs=[any_space] * len(shapes),
        scratch_shapes=scratch,
        input_output_aliases=aliases,
        compiler_params=pltpu.CompilerParams(collective_id=cid, has_side_effects=True),
        name=f"exchange_{cid}",
    )(*sources, *extra)


def solution(mesh):
    sizes = {name: mesh.shape[name] for name in ("gx", "gy", "gz")}
    near, every = ("gx", "gy"), ("gz", "gx", "gy")

    def per_device(targets, b1, b2, b3, e1, e2, e3, noise):
        rows, cols, deep = targets.shape
        n1, n2, n3 = b1.shape[0], b2.shape[0], b3.shape[0]
        run = deep // _count(sizes, near)
        chunks = min(CHUNKS, run)
        part = run // chunks
        na, nb = n1 // _count(sizes, ("gz", "gx")), n2 // sizes["gy"]
        slab, whole, spine = (part, n1, n2), (n3, na, nb), (deep, rows, cols)
        lead = jnp.transpose(targets, (2, 0, 1))

        def forward(x):
            x = jnp.einsum("kij,jb->kib", x, b2, precision=HIGH)
            return jnp.einsum("ia,kib->kab", b1, x, precision=HIGH)

        def backward(x):
            x = jnp.einsum("kab,jb->kaj", x, b2, precision=HIGH)
            return jnp.einsum("ia,kaj->kij", b1, x, precision=HIGH)

        (x,) = exchange(sizes, 0, [(True, near, 0, 0, 0, part)], [lead], [slab])
        gathered = None
        for q in range(chunks):
            v = forward(x)
            tasks, sources, shapes = [(False, every, 0, 0, q * part, part)], [v], [whole]
            if q + 1 < chunks:
                tasks.append((True, near, 1, 1, (q + 1) * part, part))
                sources.append(lead)
                shapes.append(slab)
            got = exchange(sizes, 1 + q, tasks, sources, shapes, {} if gathered is None else {0: gathered})
            gathered = got[0]
            x = got[1] if q + 1 < chunks else None

        here = {n: lax.axis_index(n) for n in sizes}
        l1 = lax.dynamic_slice_in_dim(e1, (here["gz"] * sizes["gx"] + here["gx"]) * na, na, 0)
        l2 = lax.dynamic_slice_in_dim(e2, here["gy"] * nb, nb, 0)
        rotated = jnp.einsum("kab,kc->acb", gathered, b3, precision=HIGH)
        spectrum = l1[:, None, None] * l2[None, None, :] * e3[None, :, None] + noise[0]
        scaled = rotated / spectrum
        u = jnp.einsum("acb,kc->kab", scaled, b3, precision=HIGH)

        base = 1 + chunks
        (w,) = exchange(sizes, base, [(True, every, 0, 0, 0, part)], [u], [slab])
        result = None
        for q in range(chunks):
            y = backward(w)
            tasks, sources, shapes = [(False, near, 0, 0, q * part, part)], [y], [spine]
            if q + 1 < chunks:
                tasks.insert(0, (True, every, 1, 1, (q + 1) * part, part))
                sources.append(u)
                shapes.append(slab)
            got = exchange(sizes, base + 1 + q, tasks, sources, shapes, {} if result is None else {0: result})
            result = got[0]
            w = got[1] if q + 1 < chunks else None
        return jnp.transpose(result, (1, 2, 0))

    return jax.shard_map(
        per_device,
        mesh=mesh,
        in_specs=(P("gx", "gy", "gz"), P(), P(), P(), P(), P(), P(), P()),
        out_specs=P("gx", "gy", "gz"),
        check_vma=False,
    )
```

time: 2330 us -> 1150 us (0.49)
  blocking collectives: 1490 us -> 0 us
  Pallas kernels: 0 us -> 934 us
  waiting for transfers between devices: 361 us -> 0 us
  local copies, waits for them, and re-layouts: 235 us -> 53.2 us
  matrix products: 225 us -> 146 us
    all_to_all x5 -> x0, blocking collectives: 1490 us -> none  [the longest x1 374 us: per_device(): return lax.all_to_all(result, 'gz', split_axis=2, concat_axis=0, tiled=True)]
    pallas_call x0 -> x10, Pallas kernels: none -> 934 us  [exchange(): pl.pallas_call(body, out_shape=[jax.ShapeDtypeStruct(s, jnp.float32) for...]
    all_to_all x1 -> x0, waiting for transfers between devices: 361 us -> none  [per_device(): lax.all_to_all(block, ('gx', 'gz'), split_axis=1, concat_axis=0, tiled=True)]
    all_to_all x7 -> x0, local copies, waits for them, and re-layouts: 110 us -> none  [the longest x2 38.7 us: per_device(): block = lax.all_to_all(block, 'gy', split_axis=2, concat_axis=1, tiled=True)]
    dot_general x6 -> x18, matrix products: 225 us -> 146 us  [the longest x1 34.1 us: per_device(): rotated = jnp.einsum('kab,kc->acb', gathered, b3, precision=HIGH)]
    dot_general x4 -> x1, local copies, waits for them, and re-layouts: 73.1 us -> 16.5 us  [per_device(): u = jnp.einsum('acb,kc->kab', scaled, b3, precision=HIGH)]
  transfers between devices with their start and end apart: 1 -> 0, of which waited for: 1 -> 0; matrix products, arithmetic and copies ran while one was open for 0% -> 0% of each run, Pallas kernels for 0% -> 0%
where the time goes in v1:
time: 1150 us; the launch traced here: 1130 us
  Pallas kernels  934 us (81%)
  matrix products  146 us (13%)
  local copies, waits for them, and re-layouts  53.2 us (5%)
    pallas_call x10, Pallas kernels, exchange(): pl.pallas_call(body, out_shape=[jax.ShapeDtypeStruct(s, jnp.float32) for...  934 us
    dot_general x1, matrix products, per_device(): rotated = jnp.einsum('kab,kc->acb', gathered, b3, precision=HIGH)  34.1 us
    dot_general x4, matrix products, backward(): x = jnp.einsum('kab,jb->kaj', x, b2, precision=HIGH)  26.1 us
    dot_general x4, matrix products, forward(): x = jnp.einsum('kij,jb->kib', x, b2, precision=HIGH)  24 us

profile of v1, /device:TPU:0, one launch (start us, length us, event | category | flops | bytes accessed | tf_op | source)
XLA Modules:
  0.0 1134.5 jit_solution(11930887173730119821)
XLA Ops:
  0.0 0.0 copy-start
  0.0 17.5 %copy.15 = f32[256,128,128]{1,0,2:T(8,128)} copy(f32[256,128,128]{2,1,0:T(8,128)} %param.8) | data formatting | bytes 33554432 | tf_op args[0]
  17.5 0.0 copy-start.2
  17.5 49.8 %exchange_0.1 = f32[4,512,512]{2,1,0:T(8,128)} custom-call(f32[128,256,128]{2,1,0:T(8,128)} %bitcast.83), custom_call_target="tpu_custom_call" | custom-call | tf_op jit(solution)/shard_map/exchange_0/pallas_call | solution.py:99
  67.4 0.0 copy-done.2
  67.4 0.0 copy-start.3
  67.4 6.2 fusion.32
  73.6 0.0 copy-done.3
  73.6 5.2 convolution_bitcast_fusion.7.refs_0_
  78.8 101.8 %exchange_1.1 = (f32[512,64,128]{2,1,0:T(8,128)}, f32[4,512,512]{2,1,0:T(8,128)}) custom-call(f32[4,512,512]{2,1,0:T(8,128)} %convolution_bitcast_fusion.7.refs_0_, f32[128,256,128]{2,1,0:T(8,128)} %bitcast.84), custom_call_target="tpu_custom_call" | custom-call | tf_op jit(solution)/shard_map/exchange_1/pallas_call | solution.py:99
  180.6 6.1 fusion.30
  186.7 5.2 convolution_bitcast_fusion.6.refs_0_
  191.8 109.0 %exchange_2.1 = (f32[512,64,128]{2,1,0:T(8,128)}, f32[4,512,512]{2,1,0:T(8,128)}) custom-call(f32[4,512,512]{2,1,0:T(8,128)} %convolution_bitcast_fusion.6.refs_0_, f32[128,256,128]{2,1,0:T(8,128)} %bitcast.85, f32[512,64,128]{2,1,0:T(8,128)} %get-tuple-element.18.refs_2_), custom_call_target="tpu_custom_call", output_to_operand_aliasing={{0}: (2, {})} | custom-call | tf_op jit(solution)/shard_map/exchange_2/pallas_call | solution.py:99
  300.9 6.3 fusion.28
  307.2 5.2 convolution_bitcast_fusion.5.refs_0_
  312.4 108.4 %exchange_3.1 = (f32[512,64,128]{2,1,0:T(8,128)}, f32[4,512,512]{2,1,0:T(8,128)}) custom-call(f32[4,512,512]{2,1,0:T(8,128)} %convolution_bitcast_fusion.5.refs_0_, f32[128,256,128]{2,1,0:T(8,128)} %bitcast.86, f32[512,64,128]{2,1,0:T(8,128)} %get-tuple-element.20.refs_2_), custom_call_target="tpu_custom_call", output_to_operand_aliasing={{0}: (2, {})} | custom-call | tf_op jit(solution)/shard_map/exchange_3/pallas_call | solution.py:99
  420.8 5.3 fusion.26
  426.1 5.2 convolution_bitcast_fusion.4.refs_0_
  431.3 83.7 %exchange_4.1 = f32[512,64,128]{2,1,0:T(8,128)} custom-call(f32[4,512,512]{2,1,0:T(8,128)} %convolution_bitcast_fusion.4.refs_0_, f32[512,64,128]{2,1,0:T(8,128)} %get-tuple-element.22.refs_1_), custom_call_target="tpu_custom_call", output_to_operand_aliasing={{}: (1, {})} | custom-call | tf_op jit(solution)/shard_map/exchange_4/pallas_call | solution.py:99
  515.0 0.0 copy-done
  515.1 0.0 copy-start.4
  515.1 34.1 %fusion.1 = f32[64,128,512]{2,1,0:T(8,128)} fusion(f32[512,64,128]{2,1,0:T(8,128)} %exchange_4.1, f32[512,512]{1,0:T(8,128)S(1)} %copy-done), kind=kOutput, calls=%fused_computation.2 | convolution fusion | flops 12884901888 | bytes 34603008 | tf_op jit(solution)/shard_map/kab,kc->acb/dot_general | solution.py:149
  549.2 0.8 dynamic_slice.6
  549.9 0.8 dynamic_slice.7
  550.7 0.1 broadcast_multiply_fusion
  551.4 0.0 copy-done.4
  551.4 20.6 %fusion = f32[64,128,512]{2,1,0:T(8,128)} fusion(f32[64,128,512]{2,1,0:T(8,128)} %fusion.1, f32[]{:T(128)} %bitcast.78, f32[512]{0:T(512)S(1)} %copy-done.4, f32[64,128]{1,0:T(8,128)S(1)} %broadcast_multiply_fusion, f32[512,512]{1,0:T(8,128)S(1)} %copy-done), kind=kOutput, calls=%fused_computation.1 | convolution fusion | flops 12897484800 | bytes 34637828 | tf_op jit(solution)/shard_map/acb,kc->kab/dot_general | solution.py:152
  572.1 16.5 %copy.19 = f32[64,128,512]{1,0,2:T(8,128)} copy(f32[64,128,512]{2,1,0:T(8,128)} %fusion) | data formatting | bytes 33554432 | tf_op jit(solution)/shard_map/acb,kc->kab/dot_general | solution.py:152
  588.6 95.0 %exchange_5.1 = f32[4,512,512]{2,1,0:T(8,128)} custom-call(f32[512,64,128]{2,1,0:T(8,128)} %bitcast.79), custom_call_target="tpu_custom_call" | custom-call | tf_op jit(solution)/shard_map/exchange_5/pallas_call | solution.py:99
  683.6 6.5 fusion.24
  690.1 5.3 convolution_bitcast_fusion.3.refs_0_
  695.4 120.1 %exchange_6.1 = (f32[128,256,128]{2,1,0:T(8,128)}, f32[4,512,512]{2,1,0:T(8,128)}) custom-call(f32[4,512,512]{2,1,0:T(8,128)} %convolution_bitcast_fusion.3.refs_0_, f32[512,64,128]{2,1,0:T(8,128)} %bitcast.80), custom_call_target="tpu_custom_call" | custom-call | tf_op jit(solution)/shard_map/exchange_6/pallas_call | solution.py:99
  815.5 6.5 fusion.22
  822.1 5.1 convolution_bitcast_fusion.2.refs_0_
  827.2 108.3 %exchange_7.1 = (f32[128,256,128]{2,1,0:T(8,128)}, f32[4,512,512]{2,1,0:T(8,128)}) custom-call(f32[4,512,512]{2,1,0:T(8,128)} %convolution_bitcast_fusion.2.refs_0_, f32[512,64,128]{2,1,0:T(8,128)} %bitcast.81, f32[128,256,128]{2,1,0:T(8,128)} %get-tuple-element.24.refs_2_), custom_call_target="tpu_custom_call", output_to_operand_aliasing={{0}: (2, {})} | custom-call | tf_op jit(solution)/shard_map/exchange_7/pallas_call | solution.py:99
  935.5 6.5 fusion.20
  942.1 5.3 convolution_bitcast_fusion.1.refs_0_
  947.4 108.7 %exchange_8.1 = (f32[128,256,128]{2,1,0:T(8,128)}, f32[4,512,512]{2,1,0:T(8,128)}) custom-call(f32[4,512,512]{2,1,0:T(8,128)} %convolution_bitcast_fusion.1.refs_0_, f32[512,64,128]{2,1,0:T(8,128)} %bitcast.82, f32[128,256,128]{2,1,0:T(8,128)} %get-tuple-element.26.refs_2_), custom_call_target="tpu_custom_call", output_to_operand_aliasing={{0}: (2, {})} | custom-call | tf_op jit(solution)/shard_map/exchange_8/pallas_call | solution.py:99
  1056.1 6.5 fusion.18
  1062.7 5.0 convolution_bitcast_fusion.refs_0_
  1067.7 48.7 %exchange_9.1 = f32[128,256,128]{2,1,0:T(8,128)} custom-call(f32[4,512,512]{2,1,0:T(8,128)} %convolution_bitcast_fusion.refs_0_, f32[128,256,128]{2,1,0:T(8,128)} %get-tuple-element.28.refs_1_), custom_call_target="tpu_custom_call", output_to_operand_aliasing={{}: (1, {})} | custom-call | tf_op jit(solution)/shard_map/exchange_9/pallas_call | solution.py:99
  1116.4 0.0 copy-start.1
  1116.4 17.7 %copy.24 = f32[256,128,128]{2,1,0:T(8,128)} copy(f32[256,128,128]{1,0,2:T(8,128)} %bitcast.87) | data formatting | bytes 33554432 | tf_op jit(solution)/shard_map/transpose | solution.py:167
  1134.1 0.0 copy-done.1
Async XLA Ops:
  0.0 515.0 %copy-start = (f32[512,512]{1,0:T(8,128)S(1)}, f32[512,512]{1,0:T(8,128)}, u32[]{:S(2)}) copy-start(f32[512,512]{1,0:T(8,128)} %param.11) | copy-start | bytes 3145732
  17.5 49.8 %copy-start.2 = (f32[512,512]{1,0:T(8,128)S(1)}, f32[512,512]{1,0:T(8,128)}, u32[]{:S(2)}) copy-start(f32[512,512]{1,0:T(8,128)} %param.10) | copy-start | bytes 3145732
  67.4 6.2 copy-start.3
  515.1 36.4 %copy-start.4 = (f32[512]{0:T(512)S(1)}, f32[512]{0:T(512)}, u32[]{:S(2)}) copy-start(f32[512]{0:T(512)} %param.14) | copy-start | bytes 6148
  1116.4 17.7 %copy-start.1 = (f32[512,512]{1,0:T(8,128)S(1)}, f32[512,512]{1,0:T(8,128)}, u32[]{:S(2)}) copy-start(f32[512,512]{1,0:T(8,128)} %param.11) | copy-start | bytes 3145732
